TPU v7x, 32 devices: a whole 2x2x4 slice. The times are simulated.
32 devices in a mesh: dp: 16 (over z, y, core), tensor: 2 (over x).
Axes of the slice: x: 2, y: 2, z: 4, core: 2. Of those that a mesh axis runs over, the one named last changes fastest.
Arguments:
- training_token_input: bfloat16 [4096, 8192], P('dp', 'tensor'), may hold values from -6 to 6
- gate_output_gradient: bfloat16 [4096, 29568], P('dp', 'tensor'), may hold values from -6 to 6
- up_output_gradient: bfloat16 [4096, 29568], P('dp', 'tensor'), may hold values from -6 to 6
- gate_first_matrix: bfloat16 [8192, 64], P('tensor'), may hold values from -0.0625 to 0.0625
- gate_second_matrix: bfloat16 [64, 29568], P(None, 'tensor'), may hold values from -0.75 to 0.75
- up_first_matrix: bfloat16 [8192, 64], P('tensor'), may hold values from -0.0625 to 0.0625
- up_second_matrix: bfloat16 [64, 29568], P(None, 'tensor'), may hold values from -0.75 to 0.75
- gate_weight_base: bfloat16 [8192, 29568], P('tensor', 'dp'), may hold values from -0.0625 to 0.0625
- up_weight_base: bfloat16 [8192, 29568], P('tensor', 'dp'), may hold values from -0.0625 to 0.0625
- down_weight_base: bfloat16 [29568, 8192], P('dp', 'tensor'), may hold values from -0.03125 to 0.03125
- decode_step_input: bfloat16 [2, 512, 8192], P(None, None, 'tensor'), may hold values from -6 to 6
Outputs:
- decoded: bfloat16 [2, 512, 8192], P(None, None, 'tensor')
All inputs are finite; a program needn't handle non-finite values.
Results may differ from a plain program's by a relative error of at most 0.04.
Values may be sent and summed in bfloat16 or wider, within the bound.
A program may use at most 192 MiB of HBM per device.

v0:
```python
import math
import jax
import jax.numpy as jnp
from jax import lax
from jax.sharding import PartitionSpec as P

MODEL_WIDTH = 8192
HIDDEN_UNITS = 29568
ADAPTER_RANK = 64


def swap(value):
    return lax.ppermute(value, "tensor", ((0, 1), (1, 0)))


def pair_sum(value):
    if lax.axis_size("tensor") == 2:
        sent = value.astype(jnp.bfloat16)
        return sent.astype(jnp.float32) + swap(sent).astype(jnp.float32)
    return lax.psum(value.astype(jnp.bfloat16), "tensor").astype(jnp.float32)


def row_share(value, index):
    rows = value.shape[1] // lax.axis_size("tensor")
    return lax.dynamic_slice_in_dim(value, index * rows, rows, 1)


def on_device(
    training_token_input,
    gate_output_gradient,
    up_output_gradient,
    gate_first_matrix,
    gate_second_matrix,
    up_first_matrix,
    up_second_matrix,
    gate_weight_base,
    up_weight_base,
    down_weight_base,
    decode_step_input,
):
    f32, bf16 = (jnp.float32, jnp.bfloat16)
    n_dp, n_tensor = (lax.axis_size("dp"), lax.axis_size("tensor"))
    me = lax.axis_index("tensor")
    replica = lax.axis_index("dp")
    rank = gate_first_matrix.shape[1]
    tokens_total = training_token_input.shape[0] * n_dp
    second_learning_rate = 0.5 / math.sqrt(ADAPTER_RANK * tokens_total)
    first_learning_rate = 0.5 / math.sqrt(MODEL_WIDTH * HIDDEN_UNITS * tokens_total / ADAPTER_RANK)

    def dot(left, right, over):
        return lax.dot_general(left, right, (over, ((), ())), preferred_element_type=f32)

    firsts = jnp.concatenate([gate_first_matrix, up_first_matrix], axis=1)
    inner = jnp.concatenate(
        [
            jnp.dot(training_token_input, firsts, preferred_element_type=f32),
            dot(gate_output_gradient, gate_second_matrix, ((1,), (1,))),
            dot(up_output_gradient, up_second_matrix, ((1,), (1,))),
        ],
        axis=1,
    )
    inner = pair_sum(inner).astype(bf16)
    inner_b, inner_a = (inner[:, : 2 * rank], inner[:, 2 * rank :])
    columns = gate_weight_base.shape[1]
    group = n_dp // n_tensor
    unit = 16 * n_tensor
    padded = -(-columns // unit) * unit
    piece = padded // n_tensor
    second_gradient = jnp.concatenate(
        [
            dot(gate_output_gradient, inner_b[:, :rank], ((0,), (0,))).astype(bf16),
            dot(up_output_gradient, inner_b[:, rank:], ((0,), (0,))).astype(bf16),
        ],
        axis=1,
    )
    second_gradient = jnp.pad(
        second_gradient.reshape(group, columns, 2 * rank), ((0, 0), (0, padded - columns), (0, 0))
    ).reshape(group * padded, 2 * rank)
    first_gradient = dot(training_token_input, inner_a, ((0,), (0,))).astype(bf16)
    rows_in, second_gradient, first_gradient = lax.optimization_barrier(
        (decode_step_input, second_gradient, first_gradient)
    )
    second_gradient = lax.psum_scatter(second_gradient, "dp", scatter_dimension=0, tiled=True)
    first_gradient = lax.psum(first_gradient, "dp")

    def base(rows, weight):
        return dot(rows, weight, ((2,), (0,))).astype(bf16)

    weights = (gate_weight_base, up_weight_base)
    if n_tensor == 2:
        theirs = row_share(rows_in, 1 - me)
        ours = row_share(rows_in, me)
        arrived = [swap(base(theirs, weight)) for weight in weights]
        base_sums = [
            base(ours, weight).astype(f32) + other.astype(f32)
            for weight, other in zip(weights, arrived)
        ]
    else:
        base_sums = [
            lax.psum_scatter(
                base(rows_in, weight), "tensor", scatter_dimension=1, tiled=True
            ).astype(f32)
            for weight in weights
        ]
    start = replica // n_tensor * columns + replica % n_tensor * piece

    def old_piece(matrix):
        wide = jnp.pad(matrix, ((0, 0), (0, padded)))
        return lax.dynamic_slice_in_dim(wide, start, piece, 1).T

    old = jnp.concatenate([old_piece(gate_second_matrix), old_piece(up_second_matrix)], axis=1)
    stepped = (old.astype(f32) - second_learning_rate * second_gradient.astype(f32)).astype(bf16)
    routes = [
        ((block * n_tensor + part) * n_tensor + side, (side * group + block) * n_tensor + part)
        for block in range(group)
        for part in range(n_tensor)
        for side in range(n_tensor)
    ]
    stepped = lax.ppermute(stepped, ("dp", "tensor"), routes)
    if n_tensor == 2:
        other = swap(stepped)
        first_half = me == 0
        seconds = jnp.concatenate(
            [jnp.where(first_half, stepped, other), jnp.where(first_half, other, stepped)], axis=0
        )
    else:
        seconds = lax.all_gather(stepped, "tensor", axis=0, tiled=True)
    seconds = seconds[:columns]
    new_firsts = (firsts.astype(f32) - first_learning_rate * first_gradient.astype(f32)).astype(
        bf16
    )
    low = dot(rows_in, new_firsts, ((2,), (0,)))
    if n_tensor == 2:
        low = row_share(low, me) + swap(row_share(low, 1 - me).astype(bf16)).astype(f32)
    else:
        low = lax.psum_scatter(low.astype(bf16), "tensor", scatter_dimension=1, tiled=True).astype(
            f32
        )
    low = low.astype(bf16)
    gate = base_sums[0] + dot(low[..., :rank], seconds[:, :rank], ((2,), (1,)))
    upper = base_sums[1] + dot(low[..., rank:], seconds[:, rank:], ((2,), (1,)))
    hidden = (jax.nn.silu(gate) * upper).astype(bf16)

    def project(part):
        steps, rows, _ = part.shape
        out = dot(part, down_weight_base, ((2,), (0,))).astype(bf16)
        out = out.reshape(steps * rows, -1)
        out = lax.psum_scatter(out, "dp", scatter_dimension=0, tiled=True)
        out = lax.all_gather(out, "dp", axis=0, tiled=True)
        return out.reshape(steps, rows, -1)

    if n_tensor == 2:
        own = project(hidden)
        other = project(swap(hidden))
        share = hidden.shape[1]
        result = jnp.zeros(decode_step_input.shape[:2] + (own.shape[2],), bf16)
        result = lax.dynamic_update_slice_in_dim(result, own, me * share, 1)
        return lax.dynamic_update_slice_in_dim(result, other, (1 - me) * share, 1)
    return project(lax.all_gather(hidden, "tensor", axis=1, tiled=True))


def solution(mesh):
    placed = (
        P("dp", "tensor"),
        P("dp", "tensor"),
        P("dp", "tensor"),
        P("tensor", None),
        P(None, "tensor"),
        P("tensor", None),
        P(None, "tensor"),
        P("tensor", "dp"),
        P("tensor", "dp"),
        P("dp", "tensor"),
        P(None, None, "tensor"),
    )
    return jax.shard_map(
        on_device, mesh=mesh, in_specs=placed, out_specs=P(None, None, "tensor"), check_vma=False
    )
```

profile of v0, /device:TPU:0, one launch (start us, length us, event | category | flops | bytes accessed | tf_op | source)
XLA Modules:
  0.0 517.6 jit_solution(5538493977842545239)
XLA Ops:
  6.5 1.2 constant_dynamic-update-slice_fusion.1
  7.8 1.2 constant_dynamic-update-slice_fusion
  9.0 0.8 fusion.45
  9.9 5.0 convolution_convert_fusion.4
  14.9 0.2 copy-done.4
  15.1 1.4 convolution_convert_fusion.5
  16.6 3.0 collective-permute-start
  19.6 3.5 collective-permute-done
  23.2 3.7 fusion
  26.8 3.7 fusion.1
  30.5 1.4 fusion.20
  32.0 4.2 pad_maximum_fusion
  36.2 6.1 %copy.14 = bf16[14784,128]{1,0:T(8,128)(2,1)} copy(bf16[14784,128]{0,1:T(8,128)(2,1)} %pad_maximum_fusion) | data formatting | bytes 7569408 | tf_op jit(solution)/shard_map/concatenate | solution.py:69
  42.3 4.2 pad.11
  46.5 0.3 all-reduce.5.cloned.1.call-start
  46.8 1.2 copy-done.3
  48.0 1.2 fusion.57
  49.3 13.8 %fusion.30 = bf16[2,256,1848]{1,2,0:T(8,128)(2,1)} fusion(bf16[4096,1848]{0,1:T(8,128)(2,1)} %param.18, bf16[2,512,4096]{2,1,0:T(8,128)(2,1)} %param.21, s32[]{:T(128)S(6)} %select_n.38), kind=kOutput, calls=%fused_computation.27 | convolution fusion | flops 7752019968 | bytes 21225476 | tf_op jit(solution)/shard_map/dot_general | solution.py:51
  63.1 1.7 collective-permute-start.1
  64.8 11.7 %fusion.40 = bf16[2,256,1848]{1,2,0:T(8,128)(2,1)} fusion(bf16[4096,1848]{0,1:T(8,128)(2,1)S(1)} %bitcast.78, bf16[2,512,4096]{2,1,0:T(8,128)(2,1)} %param.21, s32[]{:T(128)S(6)} %select_n.38), kind=kOutput, calls=%fused_computation.29 | convolution fusion | flops 7752019968 | bytes 21225476 | tf_op jit(solution)/shard_map/dot_general | solution.py:51
  76.5 0.4 collective-permute-start.5
  76.9 13.6 %fusion.25 = bf16[2,256,1848]{1,2,0:T(8,128)(2,1)} fusion(bf16[4096,1848]{0,1:T(8,128)(2,1)} %param.18, bf16[2,512,4096]{2,1,0:T(8,128)(2,1)} %param.21, s32[]{:T(128)S(6)} %select_n.37), kind=kOutput, calls=%fused_computation.26 | convolution fusion | flops 7752019968 | bytes 21225476 | tf_op jit(solution)/shard_map/dot_general | solution.py:51
  90.6 27.1 %reduce-scatter.10.cloned.1.call-done = bf16[928,128]{1,0:T(8,128)(2,1)} async-done(((bf16[14848,128]{1,0:T(8,128)(2,1)}), bf16[928,128]{1,0:T(8,128)(2,1)}) %reduce-scatter.10.cloned.1.call-update) | async-done | bytes 237584
  117.7 1.1 copy.17
  118.8 0.1 subtract_convert_fusion.1
  118.9 1.1 collective-permute-start.3
  120.0 95.7 %all-reduce.5.cloned.1.call-done = bf16[4096,128]{0,1:T(8,128)(2,1)} async-done(((bf16[4096,128]{0,1:T(8,128)(2,1)}), bf16[4096,128]{0,1:T(8,128)(2,1)}) %all-reduce.5.cloned.1.call-update) | async-done | bytes 1048592 | tf_op jit(solution)/shard_map/psum | solution.py:84
  215.7 6.5 %fusion.47 = f32[2,512,128]{1,2,0:T(8,128)S(1)} fusion(bf16[2,512,4096]{2,1,0:T(8,128)(2,1)} %param.21, bf16[4096,128]{0,1:T(8,128)(2,1)} %all-reduce.5.cloned.1.call-done, bf16[4096,128]{0,1:T(8,128)(2,1)S(1)} %constant_dynamic-update-slice_fusion), kind=kOutput, calls=%fused_computation.38 | convolution fusion | flops 1076363264 | bytes 11010048 | tf_op jit(solution)/shard_map/dot_general | solution.py:51
  222.2 1.5 collective-permute-start.2
  223.8 0.6 collective-permute-start.4
  224.3 12.6 %fusion.35 = bf16[2,256,1848]{1,2,0:T(8,128)(2,1)S(1)} fusion(bf16[4096,1848]{0,1:T(8,128)(2,1)} %param.19, bf16[2,512,4096]{2,1,0:T(8,128)(2,1)} %param.21, s32[]{:T(128)S(6)} %select_n.37), kind=kOutput, calls=%fused_computation.28 | convolution fusion | flops 7752019968 | bytes 21225476 | tf_op jit(solution)/shard_map/dot_general | solution.py:51
  237.1 0.7 fusion.52
  237.9 0.6 copy-done.8
  238.5 4.8 multiply_convert_fusion
  243.3 0.2 slice-done.10
  243.5 0.7 slice-done.11
  244.2 11.3 %fusion.14 = bf16[2,256,4096]{2,1,0:T(8,128)(2,1)} fusion(bf16[2,256,1848]{1,2,0:T(8,128)(2,1)S(1)} %multiply_convert_fusion, bf16[1848,4096]{1,0:T(8,128)(2,1)S(1)} %bitcast.80), kind=kOutput, calls=%fused_computation.16 | convolution fusion | flops 7753170944 | bytes 21225472 | tf_op jit(solution)/shard_map/dot_general | solution.py:51
  255.6 1.4 copy-done.7
  257.1 1.6 collective-permute-start.6
  258.6 40.0 %collective-permute-done.6 = bf16[2,256,1848]{1,2,0:T(8,128)(2,1)S(1)} collective-permute-done((bf16[2,256,1848]{1,2,0:T(8,128)(2,1)S(1)}, bf16[2,256,1848]{1,2,0:T(8,128)(2,1)S(1)}, u32[]{:S(2)}, u32[]{:S(2)}) %collective-permute-start.6) | collective-permute-done | bytes 1892384 | tf_op jit(solution)/shard_map/ppermute | solution.py:13
  298.7 14.5 %fusion.17 = bf16[2,256,4096]{2,1,0:T(8,128)(2,1)} fusion(bf16[2,256,1848]{1,2,0:T(8,128)(2,1)S(1)} %collective-permute-done.6, bf16[1848,4096]{1,0:T(8,128)(2,1)} %param.20), kind=kOutput, calls=%fused_computation.17 | convolution fusion | flops 7753170944 | bytes 21225472 | tf_op jit(solution)/shard_map/dot_general | solution.py:51
  313.2 14.5 %reduce-scatter.6.cloned.1.call-done = bf16[32,4096]{1,0:T(8,128)(2,1)} async-done(((bf16[512,4096]{1,0:T(8,128)(2,1)}), bf16[32,4096]{1,0:T(8,128)(2,1)}) %reduce-scatter.6.cloned.1.call-update) | async-done | bytes 262160 | tf_op jit(solution)/shard_map/reduce_scatter | solution.py:148
  327.7 75.6 %reduce-scatter.8.cloned.1.call-done = bf16[32,4096]{1,0:T(8,128)(2,1)} async-done(((bf16[512,4096]{1,0:T(8,128)(2,1)}), bf16[32,4096]{1,0:T(8,128)(2,1)}) %reduce-scatter.8.cloned.1.call-update) | async-done | bytes 262160 | tf_op jit(solution)/shard_map/reduce_scatter | solution.py:148
  403.3 51.4 %all-gather.3.cloned.1.call-done = bf16[512,4096]{1,0:T(8,128)(2,1)} async-done(((bf16[32,4096]{1,0:T(8,128)(2,1)}), bf16[512,4096]{1,0:T(8,128)(2,1)}) %all-gather.3.cloned.1.call-update) | async-done | bytes 4194320 | tf_op jit(solution)/shard_map/all_gather | solution.py:149
  454.7 4.4 broadcast_in_dim.3
  459.2 2.3 constant_dynamic-update-slice_fusion.3
  461.5 44.2 %all-gather.5.cloned.1.call-done = bf16[512,4096]{1,0:T(8,128)(2,1)} async-done(((bf16[32,4096]{1,0:T(8,128)(2,1)}), bf16[512,4096]{1,0:T(8,128)(2,1)}) %all-gather.5.cloned.1.call-update) | async-done | bytes 4194320 | tf_op jit(solution)/shard_map/all_gather | solution.py:149
  505.7 4.8 constant_dynamic-update-slice_fusion.2
  (61 shorter events, 0.5 us)
Async XLA Ops:
  6.5 2.4 copy-start
  6.5 111.2 %reduce-scatter.10.cloned.1.call-start = ((), (), s32[]{:S(2)}) async-start(), calls=%async_computation.8 | async-start | bytes 4038656
  6.5 3.3 copy-start.2
  9.0 5.9 %slice-start = ((s8[7569408]{0:T(1024)(128)(4,1)}), s8[4194304]{0:T(1024)(128)(4,1)S(1)}, s32[]{:S(2)}) async-start(s8[7569408]{0:T(1024)(128)(4,1)} %bitcast.67), calls=%async_computation.9 | async-start | bytes 8388608
  9.8 5.0 slice-start.1
  9.9 5.3 %copy-start.4 = (bf16[64,14784]{1,0:T(8,128)(2,1)S(1)}, bf16[64,14784]{1,0:T(8,128)(2,1)}, u32[]{:S(2)}) copy-start(bf16[64,14784]{1,0:T(8,128)(2,1)} %param.15) | copy-start | bytes 5677060
  16.5 10.3 %slice-start.2 = ((s8[7569408]{0:T(1024)(128)(4,1)}), s8[4194304]{0:T(1024)(128)(4,1)S(1)}, s32[]{:S(2)}) async-start(s8[7569408]{0:T(1024)(128)(4,1)} %bitcast.69), calls=%async_computation.11 | async-start | bytes 8388608
  16.6 6.5 %collective-permute-start = (bf16[256,256]{0,1:T(8,128)(2,1)S(1)}, bf16[256,256]{0,1:T(8,128)(2,1)S(1)}, u32[]{:S(2)}, u32[]{:S(2)}) collective-permute-start(bf16[256,256]{0,1:T(8,128)(2,1)S(1)} %pad_maximum_fusion.2), channel_id=1, source_target_pairs={{0,1},{1,0},{2,3},{3,2},{4,5},{5,4},{6,7},{7,6},{8,9},{9,8},{10,11... | collective-permute-start | bytes 393224 | tf_op jit(solution)/shard_map/ppermute | solution.py:13
  23.1 3.7 slice-start.3
  46.5 1.5 copy-start.3
  46.5 169.2 %all-reduce.5.cloned.1.call-start = ((), (), s32[]{:S(2)}) async-start(), calls=%async_computation.3 | async-start | bytes 2097152 | tf_op jit(solution)/shard_map/psum | solution.py:84
  48.0 16.8 %slice-start.4 = ((s8[15138816]{0:T(1024)(128)(4,1)}), s8[4194304]{0:T(1024)(128)(4,1)S(1)}, s32[]{:S(2)}) async-start(s8[15138816]{0:T(1024)(128)(4,1)} %bitcast.77), calls=%async_computation.13 | async-start | bytes 8388608
  49.2 15.5 %slice-start.5 = ((s8[15138816]{0:T(1024)(128)(4,1)}), s8[4194304]{0:T(1024)(128)(4,1)S(1)}, s32[]{:S(2)}) async-start(s8[15138816]{0:T(1024)(128)(4,1)} %bitcast.77), calls=%async_computation.14 | async-start | bytes 8388608
  49.2 15.5 %slice-start.6 = ((s8[15138816]{0:T(1024)(128)(4,1)}), s8[4194304]{0:T(1024)(128)(4,1)S(1)}, s32[]{:S(2)}) async-start(s8[15138816]{0:T(1024)(128)(4,1)} %bitcast.77), calls=%async_computation.15 | async-start | bytes 8388608
  49.3 15.5 %slice-start.7 = ((s8[15138816]{0:T(1024)(128)(4,1)}), s8[2555904]{0:T(1024)(128)(4,1)S(1)}, s32[]{:S(2)}) async-start(s8[15138816]{0:T(1024)(128)(4,1)} %bitcast.77), calls=%async_computation.16 | async-start | bytes 5111808
  63.1 174.8 %collective-permute-start.1 = (bf16[2,256,1848]{1,2,0:T(8,128)(2,1)}, bf16[2,256,1848]{1,2,0:T(8,128)(2,1)}, u32[]{:S(2)}, u32[]{:S(2)}) collective-permute-start(bf16[2,256,1848]{1,2,0:T(8,128)(2,1)} %fusion.30), channel_id=1, source_target_pairs={{0,1},{1,0},{2,3},{3,2},{4,5},{5,4},{6,7},{7,6},{8,9},{9,8},{10,11... | collective-permute-start | bytes 5677064 | tf_op jit(solution)/shard_map/ppermute | solution.py:13
  76.5 161.4 %collective-permute-start.5 = (bf16[2,256,1848]{1,2,0:T(8,128)(2,1)}, bf16[2,256,1848]{1,2,0:T(8,128)(2,1)}, u32[]{:S(2)}, u32[]{:S(2)}) collective-permute-start(bf16[2,256,1848]{1,2,0:T(8,128)(2,1)} %fusion.40), channel_id=1, source_target_pairs={{0,1},{1,0},{2,3},{3,2},{4,5},{5,4},{6,7},{7,6},{8,9},{9,8},{10,11... | collective-permute-start | bytes 5677064 | tf_op jit(solution)/shard_map/ppermute | solution.py:13
  76.9 250.8 %reduce-scatter.6.cloned.1.call-start = ((), (), s32[]{:S(2)}) async-start(), calls=%async_computation.4 | async-start | bytes 4456448 | tf_op jit(solution)/shard_map/reduce_scatter | solution.py:148
  118.9 104.9 %collective-permute-start.3 = (bf16[928,128]{0,1:T(8,128)(2,1)S(1)}, bf16[928,128]{0,1:T(8,128)(2,1)S(1)}, u32[]{:S(2)}, u32[]{:S(2)}) collective-permute-start(bf16[928,128]{0,1:T(8,128)(2,1)S(1)} %subtract_convert_fusion.1), channel_id=1, source_target_pairs={{0,0},{1,16},{2,1},{3,17},{4,2},{5,18},{6,3},{7,19},{8,4},{9,20},{... | collective-permute-start | bytes 712712 | tf_op jit(solution)/shard_map/ppermute | solution.py:119
  222.2 14.7 %collective-permute-start.2 = (bf16[2,256,128]{1,2,0:T(8,128)(2,1)S(1)}, bf16[2,256,128]{1,2,0:T(8,128)(2,1)S(1)}, u32[]{:S(2)}, u32[]{:S(2)}) collective-permute-start(bf16[2,256,128]{1,2,0:T(8,128)(2,1)S(1)} %dynamic-slice_convert_fusion), channel_id=1, source_target_pairs={{0,1},{1,0},{2,3},{3,2},{4,5},{5,4},{6,7},{7,6},{8,9},{9,8},{10,11... | collective-permute-start | bytes 393224 | tf_op jit(solution)/shard_map/ppermute | solution.py:13
  223.8 13.3 %collective-permute-start.4 = (bf16[928,128]{0,1:T(8,128)(2,1)S(1)}, bf16[928,128]{0,1:T(8,128)(2,1)S(1)}, u32[]{:S(2)}, u32[]{:S(2)}) collective-permute-start(bf16[928,128]{0,1:T(8,128)(2,1)S(1)} %collective-permute-done.3), channel_id=1, source_target_pairs={{0,1},{1,0},{2,3},{3,2},{4,5},{5,4},{6,7},{7,6},{8,9},{9,8},{10,11... | collective-permute-start | bytes 712712 | tf_op jit(solution)/shard_map/ppermute | solution.py:13
  237.0 1.5 copy-start.8
  237.1 6.2 %slice-start.8 = ((s8[15138816]{0:T(1024)(128)(4,1)}), s8[4194304]{0:T(1024)(128)(4,1)S(1)}, s32[]{:S(2)}) async-start(s8[15138816]{0:T(1024)(128)(4,1)} %bitcast.79), calls=%async_computation.17 | async-start | bytes 8388608
  237.8 5.5 %slice-start.9 = ((s8[15138816]{0:T(1024)(128)(4,1)}), s8[4194304]{0:T(1024)(128)(4,1)S(1)}, s32[]{:S(2)}) async-start(s8[15138816]{0:T(1024)(128)(4,1)} %bitcast.79), calls=%async_computation.18 | async-start | bytes 8388608
  237.8 5.7 %slice-start.10 = ((s8[15138816]{0:T(1024)(128)(4,1)}), s8[4194304]{0:T(1024)(128)(4,1)S(1)}, s32[]{:S(2)}) async-start(s8[15138816]{0:T(1024)(128)(4,1)} %bitcast.79), calls=%async_computation.19 | async-start | bytes 8388608
  237.8 6.4 %slice-start.11 = ((s8[15138816]{0:T(1024)(128)(4,1)}), s8[2555904]{0:T(1024)(128)(4,1)S(1)}, s32[]{:S(2)}) async-start(s8[15138816]{0:T(1024)(128)(4,1)} %bitcast.79), calls=%async_computation.20 | async-start | bytes 5111808
  244.2 11.3 %copy-start.6 = (bf16[2,256,1848]{1,2,0:T(8,128)(2,1)}, bf16[2,256,1848]{1,2,0:T(8,128)(2,1)S(1)}, u32[]{:S(2)}) copy-start(bf16[2,256,1848]{1,2,0:T(8,128)(2,1)S(1)} %multiply_convert_fusion) | copy-start | bytes 5677060
  255.5 1.5 copy-start.7
  255.6 147.7 %reduce-scatter.8.cloned.1.call-start = ((), (), s32[]{:S(2)}) async-start(), calls=%async_computation.6 | async-start | bytes 4456448 | tf_op jit(solution)/shard_map/reduce_scatter | solution.py:148
  257.1 41.6 %collective-permute-start.6 = (bf16[2,256,1848]{1,2,0:T(8,128)(2,1)S(1)}, bf16[2,256,1848]{1,2,0:T(8,128)(2,1)S(1)}, u32[]{:S(2)}, u32[]{:S(2)}) collective-permute-start(bf16[2,256,1848]{1,2,0:T(8,128)(2,1)S(1)} %copy-done.7), channel_id=1, source_target_pairs={{0,1},{1,0},{2,3},{3,2},{4,5},{5,4},{6,7},{7,6},{8,9},{9,8},{10,11... | collective-permute-start | bytes 5677064 | tf_op jit(solution)/shard_map/ppermute | solution.py:13
  313.2 141.6 %all-gather.3.cloned.1.call-start = ((), (), s32[]{:S(2)}) async-start(), calls=%async_computation.5 | async-start | bytes 4456448 | tf_op jit(solution)/shard_map/all_gather | solution.py:149
  327.7 178.0 %all-gather.5.cloned.1.call-start = ((), (), s32[]{:S(2)}) async-start(), calls=%async_computation.7 | async-start | bytes 4456448 | tf_op jit(solution)/shard_map/all_gather | solution.py:149
  454.7 4.4 copy-start.5
  505.7 4.9 copy-start.1
Sparse Core Ops, SparseCore 0:
  46.6 71.0 reduce-scatter.9
  121.2 94.4 all-reduce.4
  255.7 71.9 reduce-scatter.5
  331.4 71.8 reduce-scatter.7
  405.3 49.3 all-gather.2
  456.8 48.8 all-gather.4
where the time goes:
time: 523 us; the launch traced here: 518 us
  waiting for transfers between devices  352 us (67%)
  matrix products  106 us (20%)
  local copies, waits for them, and re-layouts  31.1 us (6%)
  between operations  14 us (3%)
  starting transfers between devices  10.3 us (2%)
    dot_general x14, matrix products, dot(): lax.dot_general(left, right, (over, ((), ())), preferred_element_type=f32)  105 us
    psum x1, waiting for transfers between devices, on_device(): first_gradient = lax.psum(first_gradient, 'dp')  95.7 us
    all_gather x2, waiting for transfers between devices, project(): out = lax.all_gather(out, 'dp', axis=0, tiled=True)  95.6 us
    reduce_scatter x2, waiting for transfers between devices, project(): out = lax.psum_scatter(out, 'dp', scatter_dimension=0, tiled=True)  90 us
    ppermute x6, waiting for transfers between devices, swap(): return lax.ppermute(value, 'tensor', ((0, 1), (1, 0)))  43.6 us
    unnamed x7, waiting for transfers between devices  27.2 us
  transfers between devices with their start and end apart: 13, of which 8 were waited for; matrix products, arithmetic and copies ran while one was open for 16% of the time, Pallas kernels for 0%

commit v1 on v0

--- a/solution.py
+++ b/solution.py
@@ -3,6 +3,7 @@
 import jax.numpy as jnp
 from jax import lax
 from jax.sharding import PartitionSpec as P
+from jax.lax import axis_size, ppermute
 
 MODEL_WIDTH = 8192
 HIDDEN_UNITS = 29568
@@ -81,7 +82,14 @@
         (decode_step_input, second_gradient, first_gradient)
     )
     second_gradient = lax.psum_scatter(second_gradient, "dp", scatter_dimension=0, tiled=True)
-    first_gradient = lax.psum(first_gradient, "dp")
+    ndev = axis_size("dp")
+    base_arr, work_now = (first_gradient, 0)
+    while 1 << work_now < ndev:
+        r1 = tuple(((dd, dd ^ 1 << work_now) for dd in range(ndev)))
+        shaped = ppermute(base_arr, "dp", r1)
+        base_arr = base_arr + shaped
+        work_now = work_now + 1
+    first_gradient = base_arr
 
     def base(rows, weight):
         return dot(rows, weight, ((2,), (0,))).astype(bf16)

time: 523 us -> 481 us (0.920)
  waiting for transfers between devices: 352 us -> 297 us
  starting transfers between devices: 10.3 us -> 25.2 us
    psum x1 -> x0, waiting for transfers between devices: 95.7 us -> none  [on_device(): first_gradient = lax.psum(first_gradient, 'dp')]
    ppermute x0 -> x4, waiting for transfers between devices: none -> 43.6 us  [on_device(): shaped = ppermute(base_arr, 'dp', r1)]
    ppermute x1, starting transfers between devices: 1.14 us -> 9.94 us  [on_device(): stepped = lax.ppermute(stepped, ('dp', 'tensor'), routes)]
    ppermute x0 -> x4, starting transfers between devices: none -> 6.52 us  [on_device(): shaped = ppermute(base_arr, 'dp', r1)]
    unnamed x7 -> x6, waiting for transfers between devices: 27.2 us -> 22 us
  transfers between devices with their start and end apart: 13 -> 16, of which waited for: 8 -> 11; matrix products, arithmetic and copies ran while one was open for 16% -> 18% of each run, Pallas kernels for 0% -> 0%
where the time goes in v1:
time: 481 us; the launch traced here: 475 us
  waiting for transfers between devices  297 us (62%)
  matrix products  103 us (21%)
  local copies, waits for them, and re-layouts  31.7 us (7%)
  starting transfers between devices  25.2 us (5%)
  between operations  13.8 us (3%)
    dot_general x14, matrix products, dot(): lax.dot_general(left, right, (over, ((), ())), preferred_element_type=f32)  102 us
    all_gather x2, waiting for transfers between devices, project(): out = lax.all_gather(out, 'dp', axis=0, tiled=True)  95.6 us
    reduce_scatter x2, waiting for transfers between devices, project(): out = lax.psum_scatter(out, 'dp', scatter_dimension=0, tiled=True)  90.2 us
    ppermute x6, waiting for transfers between devices, swap(): return lax.ppermute(value, 'tensor', ((0, 1), (1, 0)))  45.7 us
    ppermute x4, waiting for transfers between devices, on_device(): shaped = ppermute(base_arr, 'dp', r1)  43.6 us
    unnamed x6, waiting for transfers between devices  22 us
    ppermute x1, starting transfers between devices, on_device(): stepped = lax.ppermute(stepped, ('dp', 'tensor'), routes)  9.94 us
  transfers between devices with their start and end apart: 16, of which 11 were waited for; matrix products, arithmetic and copies ran while one was open for 18% of the time, Pallas kernels for 0%

profile of v1, /device:TPU:0, one launch (start us, length us, event | category | flops | bytes accessed | tf_op | source)
XLA Modules:
  0.0 475.0 jit_solution(2607030361210206495)
XLA Ops:
  6.5 1.2 constant_dynamic-update-slice_fusion.1
  7.8 1.2 constant_dynamic-update-slice_fusion
  9.0 1.0 copy-done.6
  10.0 0.8 fusion.45
  10.8 5.0 %convolution_convert_fusion.4 = bf16[256,64]{0,1:T(8,128)(2,1)S(1)} fusion(bf16[64,14784]{1,0:T(8,128)(2,1)S(1)} %copy-done.2, bf16[256,14784]{0,1:T(8,128)(2,1)} %param.13), kind=kOutput, calls=%fused_computation.35 | convolution fusion | flops 484458496 | bytes 9494528 | tf_op jit(solution)/shard_map/dot_general | solution.py:52
  16.1 1.4 convolution_convert_fusion.5
  17.5 3.0 collective-permute-start
  20.6 3.5 collective-permute-done
  24.1 2.4 fusion
  26.6 2.4 fusion.1
  29.4 2.1 pad_maximum_fusion
  31.6 6.1 %copy.14 = bf16[14784,128]{1,0:T(8,128)(2,1)} copy(bf16[14784,128]{0,1:T(8,128)(2,1)} %pad_maximum_fusion) | data formatting | bytes 7569408 | tf_op jit(solution)/shard_map/concatenate | solution.py:70
  37.7 4.2 pad.11
  42.3 1.0 copy-done.3
  43.4 1.1 fusion.58
  44.6 1.5 add.72
  46.1 1.8 collective-permute-start.3
  48.0 14.1 %fusion.30 = bf16[2,256,1848]{1,2,0:T(8,128)(2,1)} fusion(bf16[4096,1848]{0,1:T(8,128)(2,1)} %param.18, bf16[2,512,4096]{2,1,0:T(8,128)(2,1)} %param.21, s32[]{:T(128)S(6)} %select_n.38), kind=kOutput, calls=%fused_computation.27 | convolution fusion | flops 7752019968 | bytes 21225476 | tf_op jit(solution)/shard_map/dot_general | solution.py:52
  62.0 1.5 collective-permute-start.1
  63.5 7.9 %collective-permute-done.3 = bf16[4096,128]{0,1:T(8,128)(2,1)S(1)} collective-permute-done((bf16[4096,128]{0,1:T(8,128)(2,1)S(1)}, bf16[4096,128]{0,1:T(8,128)(2,1)S(1)}, u32[]{:S(2)}, u32[]{:S(2)}) %collective-permute-start.3) | collective-permute-done | bytes 1048608 | tf_op jit(solution)/shard_map/ppermute | solution.py:89
  71.7 1.9 collective-permute-start.4
  73.6 14.4 %fusion.40 = bf16[2,256,1848]{1,2,0:T(8,128)(2,1)} fusion(bf16[4096,1848]{0,1:T(8,128)(2,1)} %param.19, bf16[2,512,4096]{2,1,0:T(8,128)(2,1)} %param.21, s32[]{:T(128)S(6)} %select_n.38), kind=kOutput, calls=%fused_computation.29 | convolution fusion | flops 7752019968 | bytes 21225476 | tf_op jit(solution)/shard_map/dot_general | solution.py:52
  87.9 1.5 collective-permute-start.9
  89.4 22.1 %collective-permute-done.4 = bf16[4096,128]{0,1:T(8,128)(2,1)S(1)} collective-permute-done((bf16[4096,128]{0,1:T(8,128)(2,1)S(1)}, bf16[4096,128]{0,1:T(8,128)(2,1)S(1)}, u32[]{:S(2)}, u32[]{:S(2)}) %collective-permute-start.4) | collective-permute-done | bytes 1048608 | tf_op jit(solution)/shard_map/ppermute | solution.py:89
  111.8 2.8 collective-permute-start.5
  114.7 11.5 %fusion.25 = bf16[2,256,1848]{1,2,0:T(8,128)(2,1)} fusion(bf16[4096,1848]{0,1:T(8,128)(2,1)S(1)} %bitcast.78, bf16[2,512,4096]{2,1,0:T(8,128)(2,1)} %param.21, s32[]{:T(128)S(6)} %select_n.37), kind=kOutput, calls=%fused_computation.26 | convolution fusion | flops 7752019968 | bytes 21225476 | tf_op jit(solution)/shard_map/dot_general | solution.py:52
  126.2 21.9 %reduce-scatter.10.cloned.1.call-done = bf16[928,128]{1,0:T(8,128)(2,1)} async-done(((bf16[14848,128]{1,0:T(8,128)(2,1)}), bf16[928,128]{1,0:T(8,128)(2,1)}) %reduce-scatter.10.cloned.1.call-update) | async-done | bytes 237584
  148.1 1.1 copy.17
  149.3 9.9 %collective-permute-start.7 = (bf16[928,128]{0,1:T(8,128)(2,1)S(1)}, bf16[928,128]{0,1:T(8,128)(2,1)S(1)}, u32[]{:S(2)}, u32[]{:S(2)}) collective-permute-start(bf16[928,128]{0,1:T(8,128)(2,1)S(1)} %subtract_convert_fusion.1), channel_id=1, source_target_pairs={{0,0},{1,16},{2,1},{3,17},{4,2},{5,18},{6,3},{7,19},{8,4},{9,20},{... | collective-permute-start | bytes 712712 | tf_op jit(solution)/shard_map/ppermute | solution.py:127
  159.2 13.4 %collective-permute-done.5 = bf16[4096,128]{0,1:T(8,128)(2,1)} collective-permute-done((bf16[4096,128]{0,1:T(8,128)(2,1)S(1)}, bf16[4096,128]{0,1:T(8,128)(2,1)}, u32[]{:S(2)}, u32[]{:S(2)}) %collective-permute-start.5) | collective-permute-done | bytes 1048608 | tf_op jit(solution)/shard_map/ppermute | solution.py:89
  172.6 6.5 %fusion.47 = f32[2,512,128]{1,2,0:T(8,128)S(1)} fusion(bf16[2,512,4096]{2,1,0:T(8,128)(2,1)} %param.21, bf16[4096,128]{0,1:T(8,128)(2,1)S(1)} %copy-done.7, bf16[4096,128]{0,1:T(8,128)(2,1)S(1)} %add.74, bf16[4096,128]{0,1:T(8,128)(2,1)} %collective-permute-done.5), kind=kOutput, calls=%fused_computation.38 | convolution fusion | flops 1076887552 | bytes 12058624 | tf_op jit(solution)/shard_map/dot_general | solution.py:52
  179.2 2.0 collective-permute-start.8
  181.2 12.6 %fusion.35 = bf16[2,256,1848]{1,2,0:T(8,128)(2,1)S(1)} fusion(bf16[4096,1848]{0,1:T(8,128)(2,1)} %param.19, bf16[2,512,4096]{2,1,0:T(8,128)(2,1)} %param.21, s32[]{:T(128)S(6)} %select_n.37), kind=kOutput, calls=%fused_computation.28 | convolution fusion | flops 7752019968 | bytes 21225476 | tf_op jit(solution)/shard_map/dot_general | solution.py:52
  194.0 0.7 fusion.53
  194.8 0.6 copy-done.10
  195.4 4.8 %multiply_convert_fusion = bf16[2,256,1848]{1,2,0:T(8,128)(2,1)S(1)} fusion(bf16[2,256,1848]{1,2,0:T(8,128)(2,1)} %collective-permute-done.9, bf16[2,256,1848]{1,2,0:T(8,128)(2,1)S(1)} %fusion.35, f32[2,256,1848]{1,2,0:T(8,128)S(1)} %fusion.53, bf16[2,256,1848]{1,2,0:T(8,128)(2,1)} %collective-permute-done.1, bf16[2,256,1848]{1,2,0:T(8,128)(2,1)S(1)} %copy-done.10, ...), kind=kOutput, calls=%fused_computation.21 | convolution fusion | flops 134830080 | bytes 13836288 | tf_op jit(solution)/shard_map/dot_general | solution.py:52
  200.4 0.7 slice-done.11
  201.1 11.3 %fusion.14 = bf16[2,256,4096]{2,1,0:T(8,128)(2,1)} fusion(bf16[2,256,1848]{1,2,0:T(8,128)(2,1)S(1)} %multiply_convert_fusion, bf16[1848,4096]{1,0:T(8,128)(2,1)S(1)} %bitcast.80), kind=kOutput, calls=%fused_computation.16 | convolution fusion | flops 7753170944 | bytes 21225472 | tf_op jit(solution)/shard_map/dot_general | solution.py:52
  212.5 1.4 copy-done.9
  214.1 42.1 %collective-permute-done.10 = bf16[2,256,1848]{1,2,0:T(8,128)(2,1)S(1)} collective-permute-done((bf16[2,256,1848]{1,2,0:T(8,128)(2,1)S(1)}, bf16[2,256,1848]{1,2,0:T(8,128)(2,1)S(1)}, u32[]{:S(2)}, u32[]{:S(2)}) %collective-permute-start.10) | collective-permute-done | bytes 1892384 | tf_op jit(solution)/shard_map/ppermute | solution.py:14
  256.3 14.3 %fusion.17 = bf16[2,256,4096]{2,1,0:T(8,128)(2,1)} fusion(bf16[2,256,1848]{1,2,0:T(8,128)(2,1)S(1)} %collective-permute-done.10, bf16[1848,4096]{1,0:T(8,128)(2,1)} %param.20), kind=kOutput, calls=%fused_computation.17 | convolution fusion | flops 7753170944 | bytes 21225472 | tf_op jit(solution)/shard_map/dot_general | solution.py:52
  270.7 14.6 %reduce-scatter.6.cloned.1.call-done = bf16[32,4096]{1,0:T(8,128)(2,1)} async-done(((bf16[512,4096]{1,0:T(8,128)(2,1)}), bf16[32,4096]{1,0:T(8,128)(2,1)}) %reduce-scatter.6.cloned.1.call-update) | async-done | bytes 262160 | tf_op jit(solution)/shard_map/reduce_scatter | solution.py:156
  285.3 75.6 %reduce-scatter.8.cloned.1.call-done = bf16[32,4096]{1,0:T(8,128)(2,1)} async-done(((bf16[512,4096]{1,0:T(8,128)(2,1)}), bf16[32,4096]{1,0:T(8,128)(2,1)}) %reduce-scatter.8.cloned.1.call-update) | async-done | bytes 262160 | tf_op jit(solution)/shard_map/reduce_scatter | solution.py:156
  361.0 51.4 %all-gather.3.cloned.1.call-done = bf16[512,4096]{1,0:T(8,128)(2,1)} async-done(((bf16[32,4096]{1,0:T(8,128)(2,1)}), bf16[512,4096]{1,0:T(8,128)(2,1)}) %all-gather.3.cloned.1.call-update) | async-done | bytes 4194320 | tf_op jit(solution)/shard_map/all_gather | solution.py:157
  412.4 4.4 broadcast_in_dim.3
  416.9 2.3 constant_dynamic-update-slice_fusion.3
  419.1 44.2 %all-gather.5.cloned.1.call-done = bf16[512,4096]{1,0:T(8,128)(2,1)} async-done(((bf16[32,4096]{1,0:T(8,128)(2,1)}), bf16[512,4096]{1,0:T(8,128)(2,1)}) %all-gather.5.cloned.1.call-update) | async-done | bytes 4194320 | tf_op jit(solution)/shard_map/all_gather | solution.py:157
  463.4 4.8 %constant_dynamic-update-slice_fusion.2 = bf16[2,512,4096]{2,1,0:T(8,128)(2,1)} fusion(bf16[2,512,4096]{2,1,0:T(8,128)(2,1)} %constant_dynamic-update-slice_fusion.3, bf16[2,256,4096]{2,1,0:T(8,128)(2,1)} %bitcast.76, s32[]{:T(128)S(6)} %select_n.38), kind=kLoop, calls=%fused_computation.67 | loop fusion | bytes 8388612 | tf_op jit(solution)/shard_map/dynamic_update_slice | solution.py:166
  (73 shorter events, 2.8 us)
Async XLA Ops:
  6.5 3.4 copy-start
  6.5 141.6 %reduce-scatter.10.cloned.1.call-start = ((), (), s32[]{:S(2)}) async-start(), calls=%async_computation.7 | async-start | bytes 4038656
  6.5 4.3 copy-start.2
  9.0 1.0 copy-start.6
  10.0 5.9 %slice-start = ((s8[7569408]{0:T(1024)(128)(4,1)}), s8[4194304]{0:T(1024)(128)(4,1)S(1)}, s32[]{:S(2)}) async-start(s8[7569408]{0:T(1024)(128)(4,1)} %bitcast.67), calls=%async_computation.8 | async-start | bytes 8388608
  10.8 5.0 %slice-start.1 = ((s8[7569408]{0:T(1024)(128)(4,1)}), s8[3375104]{0:T(1024)(128)(4,1)S(1)}, s32[]{:S(2)}) async-start(s8[7569408]{0:T(1024)(128)(4,1)} %bitcast.67), calls=%async_computation.9 | async-start | bytes 6750208
  10.8 5.3 %copy-start.4 = (bf16[64,14784]{1,0:T(8,128)(2,1)S(1)}, bf16[64,14784]{1,0:T(8,128)(2,1)}, u32[]{:S(2)}) copy-start(bf16[64,14784]{1,0:T(8,128)(2,1)} %param.15) | copy-start | bytes 5677060
  17.5 9.0 %slice-start.2 = ((s8[7569408]{0:T(1024)(128)(4,1)}), s8[4194304]{0:T(1024)(128)(4,1)S(1)}, s32[]{:S(2)}) async-start(s8[7569408]{0:T(1024)(128)(4,1)} %bitcast.69), calls=%async_computation.10 | async-start | bytes 8388608
  17.5 6.5 %collective-permute-start = (bf16[256,256]{0,1:T(8,128)(2,1)S(1)}, bf16[256,256]{0,1:T(8,128)(2,1)S(1)}, u32[]{:S(2)}, u32[]{:S(2)}) collective-permute-start(bf16[256,256]{0,1:T(8,128)(2,1)S(1)} %pad_maximum_fusion.2), channel_id=1, source_target_pairs={{0,1},{1,0},{2,3},{3,2},{4,5},{5,4},{6,7},{7,6},{8,9},{9,8},{10,11... | collective-permute-start | bytes 393224 | tf_op jit(solution)/shard_map/ppermute | solution.py:14
  24.1 2.4 slice-start.3
  41.9 1.5 copy-start.3
  41.9 2.8 collective-permute-start.2
  41.9 243.4 %reduce-scatter.6.cloned.1.call-start = ((), (), s32[]{:S(2)}) async-start(), calls=%async_computation.3 | async-start | bytes 4456448 | tf_op jit(solution)/shard_map/reduce_scatter | solution.py:156
  46.1 25.3 %collective-permute-start.3 = (bf16[4096,128]{0,1:T(8,128)(2,1)S(1)}, bf16[4096,128]{0,1:T(8,128)(2,1)S(1)}, u32[]{:S(2)}, u32[]{:S(2)}) collective-permute-start(bf16[4096,128]{0,1:T(8,128)(2,1)S(1)} %add.72), channel_id=1, source_target_pairs={{0,4},{2,6},{4,0},{6,2},{8,12},{10,14},{12,8},{14,10},{16,20},{18,... | collective-permute-start | bytes 3145736 | tf_op jit(solution)/shard_map/ppermute | solution.py:89
  62.0 132.7 %collective-permute-start.1 = (bf16[2,256,1848]{1,2,0:T(8,128)(2,1)}, bf16[2,256,1848]{1,2,0:T(8,128)(2,1)}, u32[]{:S(2)}, u32[]{:S(2)}) collective-permute-start(bf16[2,256,1848]{1,2,0:T(8,128)(2,1)} %fusion.30), channel_id=1, source_target_pairs={{0,1},{1,0},{2,3},{3,2},{4,5},{5,4},{6,7},{7,6},{8,9},{9,8},{10,11... | collective-permute-start | bytes 5677064 | tf_op jit(solution)/shard_map/ppermute | solution.py:14
  71.4 43.2 %slice-start.4 = ((s8[15138816]{0:T(1024)(128)(4,1)}), s8[2555904]{0:T(1024)(128)(4,1)S(1)}, s32[]{:S(2)}) async-start(s8[15138816]{0:T(1024)(128)(4,1)} %bitcast.77), calls=%async_computation.12 | async-start | bytes 5111808
  71.7 43.0 %slice-start.5 = ((s8[15138816]{0:T(1024)(128)(4,1)}), s8[4194304]{0:T(1024)(128)(4,1)S(1)}, s32[]{:S(2)}) async-start(s8[15138816]{0:T(1024)(128)(4,1)} %bitcast.77), calls=%async_computation.13 | async-start | bytes 8388608
  71.7 43.0 %slice-start.6 = ((s8[15138816]{0:T(1024)(128)(4,1)}), s8[4194304]{0:T(1024)(128)(4,1)S(1)}, s32[]{:S(2)}) async-start(s8[15138816]{0:T(1024)(128)(4,1)} %bitcast.77), calls=%async_computation.14 | async-start | bytes 8388608
  71.7 43.0 %slice-start.7 = ((s8[15138816]{0:T(1024)(128)(4,1)}), s8[4194304]{0:T(1024)(128)(4,1)S(1)}, s32[]{:S(2)}) async-start(s8[15138816]{0:T(1024)(128)(4,1)} %bitcast.77), calls=%async_computation.15 | async-start | bytes 8388608
  71.7 39.8 %collective-permute-start.4 = (bf16[4096,128]{0,1:T(8,128)(2,1)S(1)}, bf16[4096,128]{0,1:T(8,128)(2,1)S(1)}, u32[]{:S(2)}, u32[]{:S(2)}) collective-permute-start(bf16[4096,128]{0,1:T(8,128)(2,1)S(1)} %add.73), channel_id=1, source_target_pairs={{0,8},{2,10},{4,12},{6,14},{8,0},{10,2},{12,4},{14,6},{16,24},{18,... | collective-permute-start | bytes 3145736 | tf_op jit(solution)/shard_map/ppermute | solution.py:89
  87.9 106.9 %collective-permute-start.9 = (bf16[2,256,1848]{1,2,0:T(8,128)(2,1)}, bf16[2,256,1848]{1,2,0:T(8,128)(2,1)}, u32[]{:S(2)}, u32[]{:S(2)}) collective-permute-start(bf16[2,256,1848]{1,2,0:T(8,128)(2,1)} %fusion.40), channel_id=1, source_target_pairs={{0,1},{1,0},{2,3},{3,2},{4,5},{5,4},{6,7},{7,6},{8,9},{9,8},{10,11... | collective-permute-start | bytes 5677064 | tf_op jit(solution)/shard_map/ppermute | solution.py:14
  111.8 60.8 %copy-start.7 = (bf16[4096,128]{0,1:T(8,128)(2,1)S(1)}, bf16[4096,128]{0,1:T(8,128)(2,1)}, u32[]{:S(2)}) copy-start(bf16[4096,128]{0,1:T(8,128)(2,1)} %copy-done.6) | copy-start | bytes 3145732
  111.8 60.8 %collective-permute-start.5 = (bf16[4096,128]{0,1:T(8,128)(2,1)S(1)}, bf16[4096,128]{0,1:T(8,128)(2,1)}, u32[]{:S(2)}, u32[]{:S(2)}) collective-permute-start(bf16[4096,128]{0,1:T(8,128)(2,1)S(1)} %add.74), channel_id=1, source_target_pairs={{0,16},{2,18},{4,20},{6,22},{8,24},{10,26},{12,28},{14,30},{16,0},... | collective-permute-start | bytes 3145736 | tf_op jit(solution)/shard_map/ppermute | solution.py:89
  149.3 30.0 %collective-permute-start.7 = (bf16[928,128]{0,1:T(8,128)(2,1)S(1)}, bf16[928,128]{0,1:T(8,128)(2,1)S(1)}, u32[]{:S(2)}, u32[]{:S(2)}) collective-permute-start(bf16[928,128]{0,1:T(8,128)(2,1)S(1)} %subtract_convert_fusion.1), channel_id=1, source_target_pairs={{0,0},{1,16},{2,1},{3,17},{4,2},{5,18},{6,3},{7,19},{8,4},{9,20},{... | collective-permute-start | bytes 712712 | tf_op jit(solution)/shard_map/ppermute | solution.py:127
  179.2 14.8 %collective-permute-start.6 = (bf16[2,256,128]{1,2,0:T(8,128)(2,1)S(1)}, bf16[2,256,128]{1,2,0:T(8,128)(2,1)S(1)}, u32[]{:S(2)}, u32[]{:S(2)}) collective-permute-start(bf16[2,256,128]{1,2,0:T(8,128)(2,1)S(1)} %dynamic-slice_convert_fusion), channel_id=1, source_target_pairs={{0,1},{1,0},{2,3},{3,2},{4,5},{5,4},{6,7},{7,6},{8,9},{9,8},{10,11... | collective-permute-start | bytes 393224 | tf_op jit(solution)/shard_map/ppermute | solution.py:14
  179.2 14.7 %collective-permute-start.8 = (bf16[928,128]{0,1:T(8,128)(2,1)S(1)}, bf16[928,128]{0,1:T(8,128)(2,1)S(1)}, u32[]{:S(2)}, u32[]{:S(2)}) collective-permute-start(bf16[928,128]{0,1:T(8,128)(2,1)S(1)} %collective-permute-done.7), channel_id=1, source_target_pairs={{0,1},{1,0},{2,3},{3,2},{4,5},{5,4},{6,7},{7,6},{8,9},{9,8},{10,11... | collective-permute-start | bytes 712712 | tf_op jit(solution)/shard_map/ppermute | solution.py:14
  193.9 1.5 copy-start.10
  194.0 6.2 %slice-start.8 = ((s8[15138816]{0:T(1024)(128)(4,1)}), s8[4194304]{0:T(1024)(128)(4,1)S(1)}, s32[]{:S(2)}) async-start(s8[15138816]{0:T(1024)(128)(4,1)} %bitcast.79), calls=%async_computation.16 | async-start | bytes 8388608
  194.7 5.5 %slice-start.9 = ((s8[15138816]{0:T(1024)(128)(4,1)}), s8[4194304]{0:T(1024)(128)(4,1)S(1)}, s32[]{:S(2)}) async-start(s8[15138816]{0:T(1024)(128)(4,1)} %bitcast.79), calls=%async_computation.17 | async-start | bytes 8388608
  194.8 5.7 %slice-start.10 = ((s8[15138816]{0:T(1024)(128)(4,1)}), s8[4194304]{0:T(1024)(128)(4,1)S(1)}, s32[]{:S(2)}) async-start(s8[15138816]{0:T(1024)(128)(4,1)} %bitcast.79), calls=%async_computation.18 | async-start | bytes 8388608
  194.8 6.4 %slice-start.11 = ((s8[15138816]{0:T(1024)(128)(4,1)}), s8[2555904]{0:T(1024)(128)(4,1)S(1)}, s32[]{:S(2)}) async-start(s8[15138816]{0:T(1024)(128)(4,1)} %bitcast.79), calls=%async_computation.19 | async-start | bytes 5111808
  201.1 11.3 %copy-start.8 = (bf16[2,256,1848]{1,2,0:T(8,128)(2,1)}, bf16[2,256,1848]{1,2,0:T(8,128)(2,1)S(1)}, u32[]{:S(2)}) copy-start(bf16[2,256,1848]{1,2,0:T(8,128)(2,1)S(1)} %multiply_convert_fusion) | copy-start | bytes 5677060
  212.5 1.5 copy-start.9
  212.5 148.5 %reduce-scatter.8.cloned.1.call-start = ((), (), s32[]{:S(2)}) async-start(), calls=%async_computation.5 | async-start | bytes 4456448 | tf_op jit(solution)/shard_map/reduce_scatter | solution.py:156
  214.0 42.3 %collective-permute-start.10 = (bf16[2,256,1848]{1,2,0:T(8,128)(2,1)S(1)}, bf16[2,256,1848]{1,2,0:T(8,128)(2,1)S(1)}, u32[]{:S(2)}, u32[]{:S(2)}) collective-permute-start(bf16[2,256,1848]{1,2,0:T(8,128)(2,1)S(1)} %copy-done.9), channel_id=1, source_target_pairs={{0,1},{1,0},{2,3},{3,2},{4,5},{5,4},{6,7},{7,6},{8,9},{9,8},{10,11... | collective-permute-start | bytes 5677064 | tf_op jit(solution)/shard_map/ppermute | solution.py:14
  270.6 141.8 %all-gather.3.cloned.1.call-start = ((), (), s32[]{:S(2)}) async-start(), calls=%async_computation.4 | async-start | bytes 4456448 | tf_op jit(solution)/shard_map/all_gather | solution.py:157
  285.3 178.1 %all-gather.5.cloned.1.call-start = ((), (), s32[]{:S(2)}) async-start(), calls=%async_computation.6 | async-start | bytes 4456448 | tf_op jit(solution)/shard_map/all_gather | solution.py:157
  412.4 4.4 copy-start.5
  463.4 4.9 %copy-start.1 = (bf16[256,4096]{1,0:T(8,128)(2,1)S(1)}, bf16[256,4096]{1,0:T(8,128)(2,1)}, u32[]{:S(2)}) copy-start(bf16[256,4096]{1,0:T(8,128)(2,1)} %param.11) | copy-start | bytes 6291460
Sparse Core Ops, SparseCore 0:
  42.0 106.0 reduce-scatter.9
  212.6 72.5 reduce-scatter.5
  289.1 71.8 reduce-scatter.7
  363.0 49.3 all-gather.2
  414.4 48.8 all-gather.4
